TPU v7x, 32 devices: a whole 2x2x4 slice. The times are simulated.
32 devices in a mesh: batch: 4 (over x, core), lat: 8 (over z, y).
Axes of the slice: x: 2, y: 2, z: 4, core: 2. Of those that a mesh axis runs over, the one named last changes fastest.
Arguments:
- predicted: bfloat16 [4, 73, 192, 1440], P('batch', None, 'lat'), may hold values from -64 to 64
- target: bfloat16 [4, 73, 192, 1440], P('batch', None, 'lat'), may hold values from -128 to 128
- legendre_basis: bfloat16 [192, 96, 720], P(None, ('batch', 'lat')), may hold values from -1 to 1
Outputs:
- spectra: float32 [2, 73, 720], replicated
- channel_loss: float32 [73], replicated
All inputs are finite; a program needn't handle non-finite values.
Results may differ from a plain program's by a relative error of at most 0.0003.
Values may be sent and summed in bfloat16 or wider, within the bound.
No kernel may reach another device: no remote copies, remote signals or barrier semaphores. Data moves between devices by JAX's collectives and lax.ppermute only.
A program may use at most 128 MiB of HBM per device.

v0:
```python
import math
import jax
import jax.numpy as jnp
from jax import lax
from jax.sharding import PartitionSpec as P


def fourier_table(lon_count, order_count):
    lon_ids = jnp.arange(lon_count, dtype=jnp.int32)
    order_ids = jnp.arange(order_count, dtype=jnp.int32)
    product_ids = lon_ids[:, None] * order_ids[None, :] % lon_count
    angles = 2.0 * math.pi / lon_count * product_ids.astype(jnp.float32)
    inv_root = 1.0 / math.sqrt(lon_count)
    return jnp.stack([jnp.cos(angles) * inv_root, -jnp.sin(angles) * inv_root], axis=1).astype(
        jnp.bfloat16
    )


def band_energy(fourier, basis_block, orders):
    coefficients = jnp.einsum(
        "fpmbcn,nml->fpmbcl", fourier, basis_block, preferred_element_type=jnp.float32
    )
    squares = jnp.sum(coefficients * coefficients, axis=1)
    weights = jnp.where(orders == 0, 1.0, 2.0).astype(jnp.float32)
    return jnp.sum(squares * weights[None, :, None, None, None], axis=(1, 2))


def body(predicted, target, legendre_basis):
    groups = lax.axis_size("batch")
    band_count = lax.axis_size("lat")
    per_dev = legendre_basis.shape[1]
    order_count = per_dev * groups * band_count
    dft_table = fourier_table(predicted.shape[3], order_count)
    band_id = lax.axis_index("lat")

    def transform(field_in):
        return jnp.einsum(
            "bcnk,kpm->pmbcn", field_in, dft_table, preferred_element_type=jnp.float32
        ).astype(jnp.bfloat16)

    fourier = jnp.stack([transform(predicted), transform(target)], axis=0)
    members = fourier.shape[3]
    channels = fourier.shape[4]
    lat_rows = fourier.shape[5]
    fourier = fourier.reshape(2, 2, groups, band_count, per_dev, members, channels, lat_rows)
    arrived = lax.all_to_all(fourier, "lat", split_axis=3, concat_axis=7, tiled=True)
    arrived = arrived.reshape(
        2, 2, groups * per_dev, arrived.shape[5], arrived.shape[6], arrived.shape[7]
    )
    basis_block = lax.all_gather(legendre_basis, "batch", axis=1, tiled=True)
    taken = basis_block.shape[1]
    gathered_ids = jnp.arange(taken, dtype=jnp.int32)
    orders = (
        gathered_ids // per_dev * band_count * per_dev + band_id * per_dev + gathered_ids % per_dev
    )
    partial_value = band_energy(arrived, basis_block, orders)
    energy = lax.psum(partial_value, "lat")
    energy = lax.psum(energy, "batch")
    spectra = energy / (predicted.shape[0] * groups * order_count)
    log_spectra = jnp.log(spectra + 1e-06)
    channel_loss = jnp.mean((log_spectra[0] - log_spectra[1]) ** 2, axis=1)
    return (spectra, channel_loss)


def solution(mesh):
    placed = (
        P("batch", None, "lat", None),
        P("batch", None, "lat", None),
        P(None, ("batch", "lat"), None),
    )
    return jax.shard_map(body, mesh=mesh, in_specs=placed, out_specs=(P(), P()), check_vma=False)
```

profile of v0, /device:TPU:0, one launch (start us, length us, event | category | flops | bytes accessed | tf_op | source)
XLA Modules:
  0.0 212.2 jit_solution(11625327290755649896)
XLA Ops:
  7.2 0.0 all-gather.2.cloned.1.call-start
  7.2 0.7 all-gather.2.cloned.1.call-update
  7.9 2.6 %multiply_convert_fusion = (bf16[1440,1,96]{0,2,1:T(8,128)(2,1)S(1)}, bf16[1440,1,96]{0,2,1:T(8,128)(2,1)S(1)}) fusion(), kind=kLoop, calls=%fused_computation.17 | loop fusion | flops 1935360 | bytes 552960 | tf_op jit(solution)/shard_map/convert.1
  10.5 0.0 copy-start
  10.5 0.0 copy-start.1
  10.5 0.7 copy-done
  11.2 0.1 copy-done.1
  11.3 4.8 %fusion.8 = bf16[2,96,73,24]{1,2,3,0:T(8,128)(2,1)S(1)} fusion(bf16[73,24,1440]{2,1,0:T(8,128)(2,1)} %bitcast.33, bf16[1440,1,96]{0,2,1:T(8,128)(2,1)S(1)} %get-tuple-element.4, bf16[1440,1,96]{0,2,1:T(8,128)(2,1)S(1)} %get-tuple-element.5), kind=kOutput, calls=%fused_computation.11 | convolution fusion | flops 970228224 | bytes 6271488 | tf_op jit(solution)/shard_map/bcnk,kpm->pmbcn/dot_general | solution.py:37
  16.1 0.9 copy.29
  17.0 5.5 %fusion.11 = bf16[2,96,73,24]{1,2,3,0:T(8,128)(2,1)S(1)} fusion(bf16[73,24,1440]{2,1,0:T(8,128)(2,1)} %bitcast.34, bf16[1440,1,96]{0,2,1:T(8,128)(2,1)} %copy-done, bf16[1440,1,96]{0,2,1:T(8,128)(2,1)} %copy-done.1), kind=kOutput, calls=%fused_computation.12 | convolution fusion | flops 970228224 | bytes 6271488 | tf_op jit(solution)/shard_map/bcnk,kpm->pmbcn/dot_general | solution.py:37
  22.5 0.9 copy.31
  23.3 0.5 pad_maximum_fusion
  23.9 2.0 copy.32
  25.9 7.5 %all-to-all-start = ((bf16[2,2,4,8,3,1,73,24]{6,7,4,2,1,5,0,3:T(8,128)(2,1)}), bf16[2,2,4,8,3,1,73,24]{6,7,4,2,1,5,0,3:T(8,128)(2,1)S(1)}, u32[]{:S(2)}, u32[]{:S(2)}) async-start(bf16[2,2,4,8,3,1,73,24]{6,7,4,2,1,5,0,3:T(8,128)(2,1)} %copy.32), calls=%async_computation | async-start | bytes 4718592 | tf_op jit(solution)/shard_map/all_to_all | solution.py:46
  33.5 0.0 all-reduce.3.cloned.1.call-start
  33.5 53.6 %all-to-all-done = bf16[2,2,4,8,3,1,73,24]{6,7,4,2,1,5,0,3:T(8,128)(2,1)S(1)} async-done(((bf16[2,2,4,8,3,1,73,24]{6,7,4,2,1,5,0,3:T(8,128)(2,1)}), bf16[2,2,4,8,3,1,73,24]{6,7,4,2,1,5,0,3:T(8,128)(2,1)S(1)}, u32[]{:S(2)}, u32[]{:S(2)}) %all-to-all-start) | async-done | bytes 1345568 | tf_op jit(solution)/shard_map/all_to_all | solution.py:46
  87.1 2.1 copy.33
  89.2 0.0 all-gather.2.cloned.1.call-done
  89.2 5.1 %multiply_reduce_fusion = f32[12,2,73,720]{3,2,1,0:T(8,128)S(1)} fusion(bf16[192,12,720]{2,0,1:T(8,128)(2,1)} %all-gather.2.cloned.1.call-done, bf16[2,2,12,73,192]{3,4,2,1,0:T(8,128)(2,1)} %bitcast.30), kind=kOutput, calls=%fused_computation | convolution fusion | flops 972570240 | bytes 9709056 | tf_op jit(solution)/shard_map/fpmbcn,nml->fpmbcl/dot_general | solution.py:20
  94.3 0.6 multiply_reduce_fusion.1
  94.9 1.1 copy.40
  96.0 0.0 all-reduce.3.cloned.1.call-update
  96.1 0.0 all-reduce.5.cloned.1.call-start
  96.1 71.4 %all-reduce.3.cloned.1.call-done = f32[2,73,720]{2,0,1:T(2,128)} async-done(((f32[2,73,720]{2,0,1:T(2,128)}), f32[2,73,720]{2,0,1:T(2,128)}) %all-reduce.3.cloned.1.call-update) | async-done | bytes 420496 | tf_op jit(solution)/shard_map/psum | solution.py:57
  167.5 0.0 all-reduce.5.cloned.1.call-update
  167.6 34.7 %all-reduce.5.cloned.1.call-done = f32[2,73,720]{2,0,1:T(2,128)} async-done(((f32[2,73,720]{2,0,1:T(2,128)}), f32[2,73,720]{2,0,1:T(2,128)}) %all-reduce.5.cloned.1.call-update) | async-done | bytes 420496 | tf_op jit(solution)/shard_map/psum | solution.py:58
  202.2 2.2 %add_log_fusion = (f32[2,73,720]{2,0,1:T(2,128)S(1)}, f32[2,73,720]{2,0,1:T(2,128)}) fusion(f32[2,73,720]{2,0,1:T(2,128)} %all-reduce.5.cloned.1.call-done), kind=kLoop, calls=%fused_computation.23 | loop fusion | flops 210240 | bytes 1261440 | tf_op jit(solution)/shard_map/log | solution.py:60
  204.5 0.6 fusion.20
  205.1 0.5 broadcast_multiply_fusion.1
  (1 shorter events, 0.0 us)
Async XLA Ops:
  7.2 82.1 %all-gather.2.cloned.1.call-start = ((), (), s32[]{:S(2)}) async-start(), calls=%async_computation.1 | async-start | bytes 4423680 | tf_op jit(solution)/shard_map/all_gather | solution.py:50
  10.5 0.7 copy-start
  10.5 0.8 copy-start.1
  25.9 61.2 %all-to-all-start = ((bf16[2,2,4,8,3,1,73,24]{6,7,4,2,1,5,0,3:T(8,128)(2,1)}), bf16[2,2,4,8,3,1,73,24]{6,7,4,2,1,5,0,3:T(8,128)(2,1)S(1)}, u32[]{:S(2)}, u32[]{:S(2)}) async-start(bf16[2,2,4,8,3,1,73,24]{6,7,4,2,1,5,0,3:T(8,128)(2,1)} %copy.32), calls=%async_computation | async-start | bytes 4718592 | tf_op jit(solution)/shard_map/all_to_all | solution.py:46
  33.5 134.1 %all-reduce.3.cloned.1.call-start = ((), (), s32[]{:S(2)}) async-start(), calls=%async_computation.2 | async-start | bytes 897024 | tf_op jit(solution)/shard_map/psum | solution.py:57
  96.1 106.2 %all-reduce.5.cloned.1.call-start = ((), (), s32[]{:S(2)}) async-start(), calls=%async_computation.3 | async-start | bytes 897024 | tf_op jit(solution)/shard_map/psum | solution.py:58
Sparse Core Ops, SparseCore 0:
  9.5 33.4 all-gather.1
  96.2 71.2 all-reduce.2
  169.9 32.2 all-reduce.4
where the time goes:
time: 212 us
  waiting for transfers between devices  160 us (75%)
  matrix products  15.4 us (7%)
  between operations  13.8 us (7%)
  local copies, waits for them, and re-layouts  7.77 us (4%)
  starting transfers between devices  7.66 us (4%)
  other arithmetic  7.07 us (3%)
    psum x1, waiting for transfers between devices, body(): energy = lax.psum(partial_value, 'lat')  71.4 us
    all_to_all x1, waiting for transfers between devices, body(): lax.all_to_all(fourier, 'lat', split_axis=3, concat_axis=7, tiled=True)  53.6 us
    psum x1, waiting for transfers between devices, body(): energy = lax.psum(energy, 'batch')  34.7 us
    dot_general x2, matrix products, transform(): jnp.einsum('bcnk,kpm->pmbcn', field_in, dft_table, preferred_element_type...  10.3 us
    all_to_all x1, starting transfers between devices, body(): lax.all_to_all(fourier, 'lat', split_axis=3, concat_axis=7, tiled=True)  7.55 us
    dot_general x1, matrix products, band_energy(): jnp.einsum('fpmbcn,nml->fpmbcl', fourier, basis_block, preferred_element_...  5.1 us
  transfers between devices with their start and end apart: 4, of which 3 were waited for; matrix products, arithmetic and copies ran while one was open for 9% of the time, Pallas kernels for 0%

commit v1 on v0

--- a/solution.py
+++ b/solution.py
@@ -43,7 +43,10 @@
     channels = fourier.shape[4]
     lat_rows = fourier.shape[5]
     fourier = fourier.reshape(2, 2, groups, band_count, per_dev, members, channels, lat_rows)
-    arrived = lax.all_to_all(fourier, "lat", split_axis=3, concat_axis=7, tiled=True)
+    arrived = jnp.concatenate(
+        lax.all_to_all(jnp.stack(jnp.split(fourier, lax.axis_size("lat"), axis=3)), "lat", 0, 0),
+        axis=7,
+    )
     arrived = arrived.reshape(
         2, 2, groups * per_dev, arrived.shape[5], arrived.shape[6], arrived.shape[7]
     )

time: 212 us -> 216 us (1.019)
  other arithmetic: 7.07 us -> 12.8 us
    unnamed x0 -> x7, other arithmetic: none -> 5.44 us
  transfers between devices with their start and end apart: 4 -> 4, of which waited for: 3 -> 3; matrix products, arithmetic and copies ran while one was open for 9% -> 11% of each run, Pallas kernels for 0% -> 0%
where the time goes in v1:
time: 216 us
  waiting for transfers between devices  160 us (74%)
  matrix products  15.4 us (7%)
  between operations  13.8 us (6%)
  other arithmetic  12.8 us (6%)
  starting transfers between devices  7.66 us (4%)
  local copies, waits for them, and re-layouts  5.73 us (3%)
    psum x1, waiting for transfers between devices, body(): energy = lax.psum(partial_value, 'lat')  71.4 us
    all_to_all x1, waiting for transfers between devices, body(): lax.all_to_all(jnp.stack(jnp.split(fourier, lax.axis_size('lat'), axis=3)...  53.6 us
    psum x1, waiting for transfers between devices, body(): energy = lax.psum(energy, 'batch')  34.7 us
    dot_general x2, matrix products, transform(): jnp.einsum('bcnk,kpm->pmbcn', field_in, dft_table, preferred_element_type...  10.3 us
    all_to_all x1, starting transfers between devices, body(): lax.all_to_all(jnp.stack(jnp.split(fourier, lax.axis_size('lat'), axis=3)...  7.55 us
    unnamed x7, other arithmetic  5.44 us
    dot_general x1, matrix products, band_energy(): jnp.einsum('fpmbcn,nml->fpmbcl', fourier, basis_block, preferred_element_...  5.1 us
  transfers between devices with their start and end apart: 4, of which 3 were waited for; matrix products, arithmetic and copies ran while one was open for 11% of the time, Pallas kernels for 0%

profile of v1, /device:TPU:0, one launch (start us, length us, event | category | flops | bytes accessed | tf_op | source)
XLA Modules:
  0.0 215.8 jit_solution(8403773858691226363)
XLA Ops:
  7.2 0.0 all-gather.2.cloned.1.call-start
  7.2 0.7 all-gather.2.cloned.1.call-update
  7.9 2.6 %multiply_convert_fusion = (bf16[1440,1,96]{0,2,1:T(8,128)(2,1)S(1)}, bf16[1440,1,96]{0,2,1:T(8,128)(2,1)S(1)}) fusion(), kind=kLoop, calls=%fused_computation.30 | loop fusion | flops 1935360 | bytes 552960 | tf_op jit(solution)/shard_map/convert.1
  10.5 0.7 copy-done
  11.2 0.1 copy-done.1
  11.3 4.8 %fusion.8 = bf16[2,96,73,24]{1,2,3,0:T(8,128)(2,1)S(1)} fusion(bf16[73,24,1440]{2,1,0:T(8,128)(2,1)} %bitcast.77, bf16[1440,1,96]{0,2,1:T(8,128)(2,1)S(1)} %get-tuple-element.4, bf16[1440,1,96]{0,2,1:T(8,128)(2,1)S(1)} %get-tuple-element.5), kind=kOutput, calls=%fused_computation.24 | convolution fusion | flops 970228224 | bytes 6271488 | tf_op jit(solution)/shard_map/bcnk,kpm->pmbcn/dot_general | solution.py:37
  16.1 0.9 copy.55
  17.0 5.5 %fusion.11 = bf16[2,96,73,24]{1,2,3,0:T(8,128)(2,1)S(1)} fusion(bf16[73,24,1440]{2,1,0:T(8,128)(2,1)} %bitcast.78, bf16[1440,1,96]{0,2,1:T(8,128)(2,1)} %copy-done, bf16[1440,1,96]{0,2,1:T(8,128)(2,1)} %copy-done.1), kind=kOutput, calls=%fused_computation.25 | convolution fusion | flops 970228224 | bytes 6271488 | tf_op jit(solution)/shard_map/bcnk,kpm->pmbcn/dot_general | solution.py:37
  22.5 0.9 copy.57
  23.3 0.8 bitcast_dynamic-update-slice_fusion.5
  24.1 0.8 bitcast_dynamic-update-slice_fusion.4
  24.9 0.8 bitcast_dynamic-update-slice_fusion.3
  25.7 0.8 bitcast_dynamic-update-slice_fusion.2
  26.5 0.8 bitcast_dynamic-update-slice_fusion.1
  27.2 0.8 bitcast_dynamic-update-slice_fusion
  28.0 0.8 bitcast_dynamic-update-slice_fusion.6
  28.8 0.8 fusion.27
  29.6 7.5 %all-to-all-start = ((bf16[8,2,2,4,1,3,1,73,24]{7,8,5,3,2,1,6,4,0:T(8,128)(2,1)}), bf16[8,2,2,4,1,3,1,73,24]{7,8,5,3,2,1,6,4,0:T(8,128)(2,1)S(1)}, u32[]{:S(2)}, u32[]{:S(2)}) async-start(bf16[8,2,2,4,1,3,1,73,24]{7,8,5,3,2,1,6,4,0:T(8,128)(2,1)} %fusion.27), calls=%async_computation | async-start | bytes 4718592 | tf_op jit(solution)/shard_map/all_to_all | solution.py:47
  37.1 0.0 all-reduce.3.cloned.1.call-start
  37.2 53.6 %all-to-all-done = bf16[8,2,2,4,1,3,1,73,24]{7,8,5,3,2,1,6,4,0:T(8,128)(2,1)S(1)} async-done(((bf16[8,2,2,4,1,3,1,73,24]{7,8,5,3,2,1,6,4,0:T(8,128)(2,1)}), bf16[8,2,2,4,1,3,1,73,24]{7,8,5,3,2,1,6,4,0:T(8,128)(2,1)S(1)}, u32[]{:S(2)}, u32[]{:S(2)}) %all-to-all-start) | async-done | bytes 1345568 | tf_op jit(solution)/shard_map/all_to_all | solution.py:47
  90.8 2.1 copy.65
  92.9 5.1 %multiply_reduce_fusion = f32[12,2,73,720]{3,2,1,0:T(8,128)S(1)} fusion(bf16[192,12,720]{2,0,1:T(8,128)(2,1)} %all-gather.2.cloned.1.call-done, bf16[2,2,12,73,192]{3,4,2,1,0:T(8,128)(2,1)} %bitcast.76), kind=kOutput, calls=%fused_computation | convolution fusion | flops 972570240 | bytes 9709056 | tf_op jit(solution)/shard_map/fpmbcn,nml->fpmbcl/dot_general | solution.py:20
  98.0 0.6 multiply_reduce_fusion.1
  98.6 1.1 copy.72
  99.7 0.0 all-reduce.3.cloned.1.call-update
  99.7 0.0 all-reduce.5.cloned.1.call-start
  99.8 71.4 %all-reduce.3.cloned.1.call-done = f32[2,73,720]{2,0,1:T(2,128)} async-done(((f32[2,73,720]{2,0,1:T(2,128)}), f32[2,73,720]{2,0,1:T(2,128)}) %all-reduce.3.cloned.1.call-update) | async-done | bytes 420496 | tf_op jit(solution)/shard_map/psum | solution.py:60
  171.2 0.0 all-reduce.5.cloned.1.call-update
  171.2 34.7 %all-reduce.5.cloned.1.call-done = f32[2,73,720]{2,0,1:T(2,128)} async-done(((f32[2,73,720]{2,0,1:T(2,128)}), f32[2,73,720]{2,0,1:T(2,128)}) %all-reduce.5.cloned.1.call-update) | async-done | bytes 420496 | tf_op jit(solution)/shard_map/psum | solution.py:61
  205.9 2.2 %add_log_fusion = (f32[2,73,720]{2,0,1:T(2,128)S(1)}, f32[2,73,720]{2,0,1:T(2,128)}) fusion(f32[2,73,720]{2,0,1:T(2,128)} %all-reduce.5.cloned.1.call-done), kind=kLoop, calls=%fused_computation.36 | loop fusion | flops 210240 | bytes 1261440 | tf_op jit(solution)/shard_map/log | solution.py:63
  208.1 0.6 fusion.29
  208.8 0.5 broadcast_multiply_fusion.1
  (4 shorter events, 0.0 us)
Async XLA Ops:
  7.2 85.7 %all-gather.2.cloned.1.call-start = ((), (), s32[]{:S(2)}) async-start(), calls=%async_computation.1 | async-start | bytes 4423680 | tf_op jit(solution)/shard_map/all_gather | solution.py:53
  10.5 0.7 copy-start
  10.5 0.8 copy-start.1
  29.6 61.2 %all-to-all-start = ((bf16[8,2,2,4,1,3,1,73,24]{7,8,5,3,2,1,6,4,0:T(8,128)(2,1)}), bf16[8,2,2,4,1,3,1,73,24]{7,8,5,3,2,1,6,4,0:T(8,128)(2,1)S(1)}, u32[]{:S(2)}, u32[]{:S(2)}) async-start(bf16[8,2,2,4,1,3,1,73,24]{7,8,5,3,2,1,6,4,0:T(8,128)(2,1)} %fusion.27), calls=%async_computation | async-start | bytes 4718592 | tf_op jit(solution)/shard_map/all_to_all | solution.py:47
  37.1 134.1 %all-reduce.3.cloned.1.call-start = ((), (), s32[]{:S(2)}) async-start(), calls=%async_computation.2 | async-start | bytes 897024 | tf_op jit(solution)/shard_map/psum | solution.py:60
  99.7 106.2 %all-reduce.5.cloned.1.call-start = ((), (), s32[]{:S(2)}) async-start(), calls=%async_computation.3 | async-start | bytes 897024 | tf_op jit(solution)/shard_map/psum | solution.py:61
Sparse Core Ops, SparseCore 0:
  9.5 33.4 all-gather.1
  99.8 71.2 all-reduce.2
  173.5 32.2 all-reduce.4
